TPU v7x, 256 devices: a 4x2x16 block of a 4x16x16 slice. The times are simulated.
256 devices in a mesh: runs: 2 (over y), amp: 128 (over z, x, core).
Axes of the slice: x: 4, y: 2, z: 16, core: 2. Of those that a mesh axis runs over, the one named last changes fastest.
The devices are a block of a 4x16x16 slice.
Arguments:
- initial_state: float32 [256, 1024, 128], P(('runs', 'amp')), parts along dimension 0, may hold values from -100 to 100
- gate_angles: float32 [10, 16], P('runs'), parts along dimension 0, may hold values from -3.140625 to 3.140625
- gate_pairs: int32 [5, 16, 2], replicated, may hold values from 0 to 6, as said below
- hop_coef: float32 [23], replicated, may hold values from 0.1 to 0.4
- hop_mask: int32 [23], replicated, may hold values 0 or 1
Outputs:
- adjoint: float32 [256, 1024, 128], P(('runs', 'amp')), parts along dimension 0
- block_grads: float32 [10, 128, 128], P('runs'), parts along dimension 0
There are 2 independent parts, one for each index of `runs`. A program takes and returns all parts, laid end to end along the dimension named above; an argument that names none is the same for every part. Nothing has to cross between parts.
Inputs may be any that keep to these rules, and one draw needn't show every extreme that they name: `gate_pairs`: the two qubits of each rotation differ.
All inputs are finite; a program needn't handle non-finite values.
Results may differ from a plain program's by a relative error of at most 0.0003.
Values sent between devices are 32-bit elements; how exact they have to be, the bound alone decides.
No kernel may reach another device: no remote copies, remote signals or barrier semaphores. Data moves between devices by JAX's collectives and lax.ppermute only.
A program may use at most 192 MiB of HBM per device.

v0:
```python
import jax
import jax.numpy as jnp
from jax import lax
from jax.sharding import Mesh
from jax.sharding import PartitionSpec as P

YQ = 3
AMP = ("amp_0", "amp_1", "amp_2")
RUNS_AMP = ("runs", "amp_0", "amp_1", "amp_2")
exact_mode = lax.Precision.HIGHEST
gram_forms = ["tci,tcj->ij", "tcia,tcja->ij", "abicd,abjcd->ij", "air,ajr->ij", "aicr,ajcr->ij"]
apply_forms = ["ij,tcj->tci", "ij,tcj->tci", "ij,abjcd->abicd", "ij,ajr->air", "ij,ajcr->aicr"]


def swapped(x, axis, bit):
    return lax.ppermute(x, axis, [(i, i ^ 1 << bit) for i in range(lax.axis_size(axis))])


def side_by_side(arrays, axis, split_dim, concat_dim, along):
    widths = [a.shape[along] for a in arrays]
    both = jnp.concatenate(arrays, axis=along)
    result = lax.all_to_all(both, axis, split_axis=split_dim, concat_axis=concat_dim, tiled=True)
    return tuple(jnp.split(result, [sum(widths[:k]) for k in range(1, len(widths))], axis=along))


def by_axis(x, axes):
    for axis in axes:
        x = lax.psum(x, axis)
    return x


def one_rotation(angle_now, pair_now, block_size):
    positions = jnp.arange(block_size, dtype=jnp.int32)
    diagonal = positions[:, None] == positions[None, :]
    one_bit = jnp.right_shift(positions, pair_now[0]) & 1
    two_bit = jnp.right_shift(positions, pair_now[1]) & 1
    flip_mask = jnp.left_shift(jnp.int32(1), pair_now[0]) | jnp.left_shift(
        jnp.int32(1), pair_now[1]
    )
    partner = jnp.bitwise_xor(positions, flip_mask)
    differ = (one_bit != two_bit)[:, None]
    zero_value = jnp.zeros((), angle_now.dtype)
    one_value = jnp.ones((), angle_now.dtype)
    sine_value = jnp.sin(angle_now)
    signed = jnp.where(one_bit < two_bit, -sine_value, sine_value)[:, None]
    rotation = jnp.where(diagonal, jnp.where(differ, jnp.cos(angle_now), one_value), zero_value)
    return rotation + jnp.where(
        differ & (positions[None, :] == partner[:, None]), signed, zero_value
    )


def build_blocks(gate_angles, gate_pairs, block_size):
    single = lambda angle_now, pair_now: one_rotation(angle_now, pair_now, block_size)
    factors = jax.vmap(jax.vmap(single))(gate_angles, gate_pairs)
    while factors.shape[1] > 1:
        factors = jnp.einsum(
            "bgij,bgjk->bgik", factors[:, 1::2], factors[:, 0::2], precision=exact_mode
        )
    return factors[:, 0]


def shaped_for(amplitudes, window):
    row_count, mid_count, lane_count = amplitudes.shape
    if window == 0:
        return amplitudes
    if window == 1:
        return amplitudes.reshape(row_count, mid_count // 4, lane_count, 4)
    if window == 2:
        stride = min(2 ** (YQ - 1), mid_count // lane_count)
        return amplitudes.reshape(
            row_count, mid_count // (stride * lane_count), lane_count, stride, lane_count
        )
    if window == 3:
        spread = lane_count // mid_count
        return amplitudes.reshape(row_count // spread, spread * mid_count, lane_count)
    return amplitudes.reshape(row_count // lane_count, lane_count, mid_count, lane_count)


def apply_local(amplitudes, unitary, window):
    row_count, mid_count, lane_count = amplitudes.shape
    if window == 1:
        widened = jnp.kron(unitary, jnp.eye(4, dtype=unitary.dtype))
        shaped = amplitudes.reshape(row_count, mid_count // 4, 4 * lane_count)
        return jnp.einsum(apply_forms[1], widened, shaped, precision=exact_mode).reshape(
            amplitudes.shape
        )
    shaped = shaped_for(amplitudes, window)
    return jnp.einsum(apply_forms[window], unitary, shaped, precision=exact_mode).reshape(
        amplitudes.shape
    )


def coupling_matrix(size, term_list, weights, dtype):
    positions = jnp.arange(size, dtype=jnp.int32)
    matrix = jnp.zeros((size, size), dtype)
    for lower, upper, slot in term_list:
        lower_bit = jnp.right_shift(positions, lower) & 1
        upper_bit = jnp.right_shift(positions, upper) & 1
        partner = jnp.bitwise_xor(positions, 1 << lower | 1 << upper)
        active = (lower_bit != upper_bit)[:, None] & (positions[None, :] == partner[:, None])
        matrix = matrix + jnp.where(active, weights[slot], jnp.zeros((), dtype))
    return matrix


def partner_half(amplitudes, local_bit, own_bit):
    flat_values = amplitudes.reshape(-1)
    total_size = flat_values.shape[0]
    shaped = flat_values.reshape(total_size // 2 ** (local_bit + 1), 2, 2**local_bit)
    return lax.dynamic_index_in_dim(shaped, 1 - own_bit, axis=1, keepdims=False)


def add_half(summed, received, scale, own_bit):
    full_shape = summed.shape
    shaped = summed.reshape(received.shape[0], 2, received.shape[1])
    present = lax.dynamic_index_in_dim(shaped, 1 - own_bit, axis=1, keepdims=True)
    updated = lax.dynamic_update_index_in_dim(
        shaped, present + scale * received[:, None, :], 1 - own_bit, axis=1
    )
    return updated.reshape(full_shape)


def hamiltonian_local(amplitudes, weights, my_index):
    row_count, mid_count, lane_count = amplitudes.shape
    full_shape = amplitudes.shape
    block_bits = lane_count.bit_length() - 1
    low_bits = mid_count.bit_length() - 1
    top_bits = row_count.bit_length() - 1
    pair_size = 2 * lane_count
    lane_terms = [(position, position + 1, position) for position in range(block_bits)]
    low_matrix = coupling_matrix(pair_size, lane_terms, weights, amplitudes.dtype)
    paired = amplitudes.reshape(row_count, mid_count // 2, pair_size)
    summed = jnp.einsum("ij,tcj->tci", low_matrix, paired, precision=exact_mode).reshape(full_shape)
    rung_base = block_bits + low_bits + top_bits - 1
    head_bits = 2 * low_bits
    head_terms = [(offset, offset + 1, block_bits + offset) for offset in range(low_bits - 1)]
    head_terms = head_terms + [
        (low_bits + offset, low_bits + offset + 1, block_bits + low_bits + offset)
        for offset in range(top_bits - 1)
        if low_bits + offset + 1 < head_bits
    ]
    head_terms = head_terms + [
        (offset, low_bits + offset, rung_base + offset) for offset in range(low_bits)
    ]
    head_matrix = coupling_matrix(2**head_bits, head_terms, weights, amplitudes.dtype)
    head_view = amplitudes.reshape(-1, 2**head_bits, lane_count)
    summed = summed + jnp.einsum(
        "ij,ajr->air", head_matrix, head_view, precision=exact_mode
    ).reshape(full_shape)
    tail_start = head_bits - 1
    tail_bits = low_bits + top_bits - tail_start
    tail_terms = [
        (
            low_bits + offset - tail_start,
            low_bits + offset + 1 - tail_start,
            block_bits + low_bits + offset,
        )
        for offset in range(top_bits - 1)
        if low_bits + offset + 1 >= head_bits
    ]
    tail_matrix = coupling_matrix(2**tail_bits, tail_terms, weights, amplitudes.dtype)
    tail_view = amplitudes.reshape(2**tail_bits, 2**tail_start, lane_count)
    summed = summed + jnp.einsum(
        "ij,jbr->ibr", tail_matrix, tail_view, precision=exact_mode
    ).reshape(full_shape)
    top_start = block_bits + low_bits
    own_first = my_index & 1
    chain_bit = block_bits + low_bits - 1
    rung_bit = top_start + low_bits
    chain_rows = partner_half(amplitudes, chain_bit, own_first)
    rung_rows = partner_half(amplitudes, rung_bit, own_first)
    chain_back, rung_back = swapped((chain_rows, rung_rows), AMP, 0)
    summed = add_half(summed, chain_back, weights[block_bits + low_bits - 1], own_first)
    summed = add_half(summed, rung_back, weights[rung_base + low_bits], own_first)
    for offset in range(1, top_bits - low_bits):
        own_bit = jnp.right_shift(my_index, offset) & 1
        far_bit = top_start + low_bits + offset
        half_rows = partner_half(amplitudes, far_bit, own_bit)
        returned = swapped(half_rows, AMP, offset)
        summed = add_half(summed, returned, weights[rung_base + low_bits + offset], own_bit)
    return summed


def on_device(initial_state, gate_angles, gate_pairs, hop_coef, hop_mask):
    lane_count = initial_state.shape[2]
    block_count = gate_angles.shape[0]
    my_index = lax.axis_index(AMP)
    weights = hop_coef * hop_mask.astype(hop_coef.dtype)
    block_stack = build_blocks(gate_angles, gate_pairs, lane_count)
    gate_blocks = [block_stack[number] for number in range(block_count)]
    factor = 2.0 / (initial_state.shape[0] * lax.axis_size(AMP) * initial_state.shape[1])
    layout = 0
    current = initial_state
    for number in range(block_count):
        window = number % 5
        wanted = 1 if window >= 3 else 0
        if wanted != layout:
            current = lax.all_to_all(current, AMP, split_axis=1, concat_axis=0, tiled=True)
            layout = wanted
        current = apply_local(current, gate_blocks[number], window)
    adjoint = hamiltonian_local(current, weights, my_index)
    collected = []
    for number in range(block_count - 1, block_count - 6, -1):
        window = number % 5
        wanted = 1 if window >= 3 else 0
        if wanted != layout:
            current, adjoint = side_by_side((current, adjoint), AMP, 0, 1, 2)
            layout = wanted
        transposed = gate_blocks[number].T
        current = apply_local(current, transposed, window)
        local_gram = jnp.einsum(
            gram_forms[window],
            shaped_for(adjoint, window),
            shaped_for(current, window),
            precision=exact_mode,
        )
        collected.append(factor * by_axis(local_gram, AMP))
        adjoint = apply_local(adjoint, transposed, window)
    block_grads = jnp.stack(collected[::-1])
    return (adjoint, block_grads)


def solution(mesh):
    split = Mesh(
        mesh.devices.reshape(mesh.shape["runs"], 16, 4, 2), ("runs", "amp_0", "amp_1", "amp_2")
    )
    return jax.shard_map(
        on_device,
        mesh=split,
        in_specs=(P(RUNS_AMP, None, None), P("runs", None), P(), P(), P()),
        out_specs=(P(RUNS_AMP, None, None), P("runs", None, None)),
        check_vma=False,
    )
```

profile of v0, /device:TPU:33, one launch (start us, length us, event | category | flops | bytes accessed | tf_op | source)
XLA Modules:
  0.0 522.9 jit_solution(7746222785642798933)
XLA Ops:
  7.2 0.8 fusion.207
  8.0 0.7 fusion.208
  9.1 5.6 %select_add_fusion = f32[5,16,128,128]{3,2,1,0:T(8,128)S(1)} fusion(f32[5,16,128]{2,1,0:T(8,128)S(1)} %get-tuple-element.22, s32[5,16,128]{2,1,0:T(8,128)S(1)} %iota_xor_fusion, f32[5,16,128]{2,1,0:T(8,128)S(1)} %get-tuple-element.21, pred[5,16,128]{2,1,0:T(8,128)(4,1)S(1)} %fusion.95, pred[128,128]{1,0:T(8,128)(4,1)S(1)} %iota_compare_fusion.8), kind=kLoop, calls=%fused_computation.2 | loop fusion | flops 6553600 | bytes 5392384 | tf_op jit(solution)/shard_map/vmap(vmap())/add | solution.py:47
  14.6 3.1 fusion.1
  17.8 1.5 fusion.4
  19.2 0.8 fusion.7
  20.6 22.0 %broadcast_multiply_fusion.1 = (f32[128,4,128,4]{3,2,1,0:T(8,128)}, f32[128,4,128,4]{3,2,1,0:T(8,128)}) fusion(f32[4,4]{1,0:T(4,128)S(1)} %fusion.178, f32[128,128]{1,0:T(8,128)S(1)} %get-tuple-element.19, f32[128,128]{1,0:T(8,128)S(1)} %copy.130), kind=kLoop, calls=%fused_computation.1 | loop fusion | flops 524288 | bytes 2228288 | tf_op jit(solution)/shard_map/jit(kron)/mul | solution.py:82
  42.6 29.0 %reshape.446 = f32[4,128,512,1]{2,1,0,3:T(8,128)S(1)} reshape(f32[128,4,128,4]{3,2,1,0:T(8,128)} %get-tuple-element.30) | data formatting | bytes 2097152 | tf_op jit(solution)/shard_map/jit(kron)/mul | solution.py:82
  72.5 1.1 fusion.22
  74.2 1.1 copy.102
  75.3 31.0 %all-to-all-start = ((f32[1,1024,128]{2,0,1:T(1,128)}), f32[1,1024,128]{2,0,1:T(1,128)S(1)}, u32[]{:S(2)}, u32[]{:S(2)}) async-start(f32[1,1024,128]{2,0,1:T(1,128)} %bitcast.16), calls=%async_computation | async-start | bytes 1048576 | tf_op jit(solution)/shard_map/all_to_all | solution.py:197
  107.2 0.7 fusion.209
  108.0 29.1 %all-to-all-done = f32[1,1024,128]{2,0,1:T(1,128)S(1)} async-done(((f32[1,1024,128]{2,0,1:T(1,128)}), f32[1,1024,128]{2,0,1:T(1,128)S(1)}, u32[]{:S(2)}, u32[]{:S(2)}) %all-to-all-start) | async-done | bytes 524320 | tf_op jit(solution)/shard_map/all_to_all | solution.py:197
  137.6 1.0 fusion.31
  138.9 1.1 reshape_reshape_reshape.16
  140.0 1.1 reshape_reshape_reshape.17
  141.1 1.1 reshape_reshape_reshape.18
  142.6 3.4 fusion.29
  146.8 5.3 %convolution_bitcast_fusion.3 = f32[16,64,128]{2,1,0:T(8,128)S(1)} fusion(f32[16,64,128]{2,1,0:T(8,128)S(1)} %bitcast.238, f32[]{:T(128)} %bitcast.52, s32[64]{0:T(128)S(1)} %get-tuple-element.65, f32[]{:T(128)} %bitcast.51, s32[64]{0:T(128)S(1)} %get-tuple-element.66, f32[]{:T(128)} %bitcast.50, s32[64]{0:T(128)S(1)} %get-tuple-element.67, f32[]{:T(128)} %bitcast.49, ...), kind=kOutput, calls=%fused_computation.14 | convolution fusion | flops 100773888 | bytes 1050844 | tf_op jit(solution)/shard_map/ij,ajr->air/dot_general | solution.py:146
  153.3 1.3 constant_dynamic-slice_fusion.2
  154.6 0.9 copy.205
  155.5 1.3 constant_dynamic-slice_fusion.1
  156.8 0.9 copy.204
  157.7 1.9 collective-permute-start.2
  159.8 0.9 copy.203
  160.7 2.9 collective-permute-start.3
  163.6 0.9 dynamic-slice_bitcast_fusion
  164.5 10.4 %collective-permute-start.4 = (f32[1,65536]{1,0:T(1,128)}, f32[1,65536]{1,0:T(1,128)}, u32[]{:S(2)}, u32[]{:S(2)}) collective-permute-start(f32[1,65536]{1,0:T(1,128)} %dynamic-slice_bitcast_fusion), channel_id=1, source_target_pairs={{0,8},{1,9},{2,10},{3,11},{4,12},{5,13},{6,14},{7,15},{8,0},{9,1},... | collective-permute-start | bytes 786440 | tf_op jit(solution)/shard_map/ppermute | solution.py:16
  175.0 5.4 %fusion.39 = f32[128,4,256]{0,2,1:T(8,128)S(1)} fusion(f32[128,4,256]{0,2,1:T(8,128)S(1)} %bitcast.241, f32[]{:T(128)} %bitcast.42, s32[256]{0:T(256)S(1)} %get-tuple-element.77, f32[]{:T(128)} %bitcast.41, s32[256]{0:T(256)S(1)} %get-tuple-element.78, f32[]{:T(128)} %bitcast.40, s32[256]{0:T(256)S(1)} %get-tuple-element.81, f32[]{:T(128)} %bitcast.39, ...), kind=kOutput, calls=%fused_computation.62 | convolution fusion | flops 404422656 | bytes 1057564 | tf_op jit(solution)/shard_map/ij,tcj->tci/dot_general | solution.py:132
  183.5 1.6 broadcast_multiply_fusion.4
  185.5 2.8 dynamic_update_slice.21
  188.9 1.6 broadcast_multiply_fusion.3
  190.9 3.3 dynamic_update_slice.22
  194.8 1.7 broadcast_multiply_fusion.2
  196.8 3.3 dynamic_update_slice.23
  200.8 2.0 bitcast_add_fusion.1
  202.8 3.3 dynamic_update_slice.24
  208.1 1.0 pad_maximum_fusion
  209.2 9.2 %all-to-all-start.1 = ((f32[128,8,256]{2,1,0:T(8,128)}), f32[128,8,256]{2,1,0:T(8,128)}, u32[]{:S(2)}, u32[]{:S(2)}) async-start(f32[128,8,256]{2,1,0:T(8,128)} %pad_maximum_fusion), calls=%async_computation.1 | async-start | bytes 2097152 | tf_op jit(solution)/shard_map/all_to_all | solution.py:22
  218.7 28.7 %mul.169 = f32[512,512]{1,0:T(8,128)S(1)} reshape(f32[128,4,128,4]{3,2,1,0:T(8,128)} %get-tuple-element.31) | data formatting | bytes 2097152 | tf_op jit(solution)/shard_map/jit(kron)/mul | solution.py:82
  247.4 1.2 convolution_bitcast_fusion.6
  248.6 1.2 convolution_bitcast_fusion.7
  249.8 19.6 %all-to-all-done.1 = f32[128,8,256]{2,1,0:T(8,128)} async-done(((f32[128,8,256]{2,1,0:T(8,128)}), f32[128,8,256]{2,1,0:T(8,128)}, u32[]{:S(2)}, u32[]{:S(2)}) %all-to-all-start.1) | async-done | bytes 1048608 | tf_op jit(solution)/shard_map/all_to_all | solution.py:22
  269.4 1.3 fusion.206
  270.7 1.0 fusion.27
  271.7 1.0 convolution_bitcast_fusion.1
  272.7 1.3 convolution_bitcast_fusion.8
  274.2 1.1 fusion.10
  275.4 0.8 reshape.440
  276.7 1.0 copy.129
  278.4 1.6 fusion.90
  280.0 1.9 fusion.13
  281.8 1.1 reshape.437
  283.0 1.3 convolution_bitcast_fusion.9
  284.3 1.6 fusion.211
  286.0 119.5 %all-reduce.7.cloned.1.call-done = (f32[128,128]{1,0:T(8,128)}, f32[128,128]{1,0:T(8,128)}, f32[128,128]{1,0:T(8,128)}, f32[128,128]{1,0:T(8,128)}, f32[128,128]{1,0:T(8,128)}) async-done(((f32[128,128]{1,0:T(8,128)}, f32[128,128]{1,0:T(8,128)}, f32[128,128]{1,0:T(8,128)}, f32[128,128]{1,0:T(8,128)}, f32[128,128]{1,0:T(8,128)}), (f32[128,128]{1,0:T(8,128)}, f32[128,128]{1,0:T(8,128)}, f32[128,128]{1,0:T(8,128)}, ...) | async-done | bytes 327696 | tf_op jit(solution)/shard_map/psum | solution.py:28
  405.6 61.8 %all-reduce.9.cloned.1.call-done = (f32[128,128]{1,0:T(8,128)}, f32[128,128]{1,0:T(8,128)}, f32[128,128]{1,0:T(8,128)}, f32[128,128]{1,0:T(8,128)}, f32[128,128]{1,0:T(8,128)}) async-done(((f32[128,128]{1,0:T(8,128)}, f32[128,128]{1,0:T(8,128)}, f32[128,128]{1,0:T(8,128)}, f32[128,128]{1,0:T(8,128)}, f32[128,128]{1,0:T(8,128)}), (f32[128,128]{1,0:T(8,128)}, f32[128,128]{1,0:T(8,128)}, f32[128,128]{1,0:T(8,128)}, ...) | async-done | bytes 327696 | tf_op jit(solution)/shard_map/psum | solution.py:28
  467.5 1.4 convolution_bitcast_fusion
  468.9 42.2 %all-reduce.11.cloned.1.call-done = (f32[128,128]{1,0:T(8,128)}, f32[128,128]{1,0:T(8,128)}, f32[128,128]{1,0:T(8,128)}, f32[128,128]{1,0:T(8,128)}, f32[128,128]{1,0:T(8,128)}) async-done(((f32[128,128]{1,0:T(8,128)}, f32[128,128]{1,0:T(8,128)}, f32[128,128]{1,0:T(8,128)}, f32[128,128]{1,0:T(8,128)}, f32[128,128]{1,0:T(8,128)}), (f32[128,128]{1,0:T(8,128)}, f32[128,128]{1,0:T(8,128)}, ...) | async-done | bytes 327696 | tf_op jit(solution)/shard_map/psum | solution.py:28
  511.1 0.8 bitcast_dynamic-update-slice_fusion.4
  511.9 0.8 bitcast_dynamic-update-slice_fusion.3
  512.8 0.8 bitcast_dynamic-update-slice_fusion.2
  513.6 0.8 bitcast_dynamic-update-slice_fusion.1
  514.4 0.8 bitcast_dynamic-update-slice_fusion
  (95 shorter events, 17.4 us)
Async XLA Ops:
  7.2 64.4 %copy-start = (f32[1,1024,128]{2,1,0:T(8,128)S(1)}, f32[1,1024,128]{2,1,0:T(8,128)}, u32[]{:S(2)}) copy-start(f32[1,1024,128]{2,1,0:T(8,128)} %param.5) | copy-start | bytes 1572868
  72.5 34.1 %copy-start.5 = (f32[23]{0:T(128)S(1)}, f32[23]{0:T(128)}, u32[]{:S(2)}) copy-start(f32[23]{0:T(128)} %param.8) | copy-start | bytes 280
  72.5 34.1 %copy-start.6 = (s32[23]{0:T(128)S(1)}, s32[23]{0:T(128)}, u32[]{:S(2)}) copy-start(s32[23]{0:T(128)} %param.9) | copy-start | bytes 280
  75.3 61.7 %all-to-all-start = ((f32[1,1024,128]{2,0,1:T(1,128)}), f32[1,1024,128]{2,0,1:T(1,128)S(1)}, u32[]{:S(2)}, u32[]{:S(2)}) async-start(f32[1,1024,128]{2,0,1:T(1,128)} %bitcast.16), calls=%async_computation | async-start | bytes 1048576 | tf_op jit(solution)/shard_map/all_to_all | solution.py:197
  152.4 7.2 %copy-start.3 = (f32[2,2,32768]{2,1,0:T(2,128)S(1)}, f32[2,2,32768]{2,1,0:T(2,128)}, u32[]{:S(2)}) copy-start(f32[2,2,32768]{2,1,0:T(2,128)} %reshape_reshape_reshape.18) | copy-start | bytes 1572868
  152.7 29.4 %collective-permute-start = (f32[128,512]{0,1:T(8,128)S(1)}, f32[128,512]{0,1:T(8,128)S(1)}, u32[]{:S(2)}, u32[]{:S(2)}) collective-permute-start(f32[128,512]{0,1:T(8,128)S(1)} %dynamic-slice_bitcast_fusion.1), channel_id=1, source_target_pairs={{0,1},{1,0},{2,3},{3,2},{4,5},{5,4},{6,7},{7,6},{8,9},{9,8},{10,11... | collective-permute-start | bytes 786440 | tf_op jit(solution)/shard_map/ppermute | solution.py:16
  155.4 28.1 %collective-permute-start.1 = (f32[8,8192]{1,0:T(8,128)}, f32[8,8192]{1,0:T(8,128)}, u32[]{:S(2)}, u32[]{:S(2)}) collective-permute-start(f32[8,8192]{1,0:T(8,128)} %bitcast.235), channel_id=1, source_target_pairs={{0,1},{1,0},{2,3},{3,2},{4,5},{5,4},{6,7},{7,6},{8,9},{9,8},{10,11... | collective-permute-start | bytes 786440 | tf_op jit(solution)/shard_map/ppermute | solution.py:16
  157.7 31.3 %collective-permute-start.2 = (f32[4,16384]{1,0:T(4,128)}, f32[4,16384]{1,0:T(4,128)}, u32[]{:S(2)}, u32[]{:S(2)}) collective-permute-start(f32[4,16384]{1,0:T(4,128)} %bitcast.234), channel_id=1, source_target_pairs={{0,2},{1,3},{2,0},{3,1},{4,6},{5,7},{6,4},{7,5},{8,10},{9,11},{10,... | collective-permute-start | bytes 786440 | tf_op jit(solution)/shard_map/ppermute | solution.py:16
  160.7 34.1 %collective-permute-start.3 = (f32[2,32768]{1,0:T(2,128)}, f32[2,32768]{1,0:T(2,128)}, u32[]{:S(2)}, u32[]{:S(2)}) collective-permute-start(f32[2,32768]{1,0:T(2,128)} %bitcast.233), channel_id=1, source_target_pairs={{0,4},{1,5},{2,6},{3,7},{4,0},{5,1},{6,2},{7,3},{8,12},{9,13},{10,... | collective-permute-start | bytes 786440 | tf_op jit(solution)/shard_map/ppermute | solution.py:16
  164.5 36.3 %collective-permute-start.4 = (f32[1,65536]{1,0:T(1,128)}, f32[1,65536]{1,0:T(1,128)}, u32[]{:S(2)}, u32[]{:S(2)}) collective-permute-start(f32[1,65536]{1,0:T(1,128)} %dynamic-slice_bitcast_fusion), channel_id=1, source_target_pairs={{0,8},{1,9},{2,10},{3,11},{4,12},{5,13},{6,14},{7,15},{8,0},{9,1},... | collective-permute-start | bytes 786440 | tf_op jit(solution)/shard_map/ppermute | solution.py:16
  209.2 60.2 %all-to-all-start.1 = ((f32[128,8,256]{2,1,0:T(8,128)}), f32[128,8,256]{2,1,0:T(8,128)}, u32[]{:S(2)}, u32[]{:S(2)}) async-start(f32[128,8,256]{2,1,0:T(8,128)} %pad_maximum_fusion), calls=%async_computation.1 | async-start | bytes 2097152 | tf_op jit(solution)/shard_map/all_to_all | solution.py:22
  218.4 187.1 %all-reduce.7.cloned.1.call-start = ((), (), s32[]{:S(2)}) async-start(), calls=%async_computation.2 | async-start | bytes 655360 | tf_op jit(solution)/shard_map/psum | solution.py:28
  277.7 2.3 copy-start.2
  281.8 234.2 %copy-start.1 = (f32[1,1024,128]{2,1,0:T(8,128)S(1)}, f32[1,1024,128]{2,1,0:T(8,128)}, u32[]{:S(2)}) copy-start(f32[1,1024,128]{2,1,0:T(8,128)} %param.5) | copy-start | bytes 1572868
  286.0 181.5 %all-reduce.9.cloned.1.call-start = ((), (), s32[]{:S(2)}) async-start(), calls=%async_computation.3 | async-start | bytes 655360 | tf_op jit(solution)/shard_map/psum | solution.py:28
  405.6 105.5 %all-reduce.11.cloned.1.call-start = ((), (), s32[]{:S(2)}) async-start(), calls=%async_computation.4 | async-start | bytes 655360 | tf_op jit(solution)/shard_map/psum | solution.py:28
  515.3 0.7 copy-start.4
Sparse Core Ops, SparseCore 0:
  286.1 119.3 all-reduce.6
  408.2 59.2 all-reduce.8
  470.4 40.5 all-reduce.10
where the time goes:
time: 532 us; the launch traced here: 523 us
  waiting for transfers between devices  272 us (51%)
  local copies, waits for them, and re-layouts  96.7 us (18%)
  starting transfers between devices  56.5 us (11%)
  other arithmetic  41.8 us (8%)
  matrix products  40.7 us (8%)
  between operations  14.9 us (3%)
    psum x3, waiting for transfers between devices, by_axis(): x = lax.psum(x, axis)  223 us
    mul x3, local copies, waits for them, and re-layouts, apply_local(): widened = jnp.kron(unitary, jnp.eye(4, dtype=unitary.dtype))  57.7 us
    all_to_all x1, starting transfers between devices, on_device(): lax.all_to_all(current, AMP, split_axis=1, concat_axis=0, tiled=True)  31 us
    all_to_all x1, waiting for transfers between devices, on_device(): lax.all_to_all(current, AMP, split_axis=1, concat_axis=0, tiled=True)  29.1 us
    mul x1, other arithmetic, apply_local(): widened = jnp.kron(unitary, jnp.eye(4, dtype=unitary.dtype))  22 us
    all_to_all x1, waiting for transfers between devices, side_by_side(): lax.all_to_all(both, axis, split_axis=split_dim, concat_axis=concat_dim,...  19.6 us
    ppermute x5, starting transfers between devices, swapped(): lax.ppermute(x, axis, [(i, i ^ 1 << bit) for i in range(lax.axis_size(axi...  15.9 us
    dynamic_update_slice x5, local copies, waits for them, and re-layouts, add_half(): lax.dynamic_update_index_in_dim(shaped, present + scale * received[:, Non...  12.9 us
  transfers between devices with their start and end apart: 10, of which 5 were waited for; matrix products, arithmetic and copies ran while one was open for 13% of the time, Pallas kernels for 0%

commit v1 on v0

--- a/solution.py
+++ b/solution.py
@@ -25,7 +25,7 @@
 
 def by_axis(x, axes):
     for axis in axes:
-        x = lax.psum(x, axis)
+        x = jnp.sum(lax.all_gather(x, axis), axis=0)
     return x
 
 

time: 532 us -> 602 us (1.13)
  blocking collectives: 0 us -> 121 us
  waiting for transfers between devices: 272 us -> 221 us
    psum x3 -> x0, waiting for transfers between devices: 223 us -> none  [by_axis(): x = lax.psum(x, axis)]
    all_gather x0 -> x5, waiting for transfers between devices: none -> 142 us  [by_axis(): x = jnp.sum(lax.all_gather(x, axis), axis=0)]
    all_gather x0 -> x10, blocking collectives: none -> 121 us  [by_axis(): x = jnp.sum(lax.all_gather(x, axis), axis=0)]
    all_to_all x1, waiting for transfers between devices: 19.6 us -> 51.8 us  [side_by_side(): lax.all_to_all(both, axis, split_axis=split_dim, concat_axis=concat_dim,...]
    reduce_sum x0 -> x15, other arithmetic: none -> 6.56 us  [by_axis(): x = jnp.sum(lax.all_gather(x, axis), axis=0)]
  transfers between devices with their start and end apart: 10 -> 12, of which waited for: 5 -> 6; matrix products, arithmetic and copies ran while one was open for 13% -> 15% of each run, Pallas kernels for 0% -> 0%
where the time goes in v1:
time: 602 us; the launch traced here: 593 us
  waiting for transfers between devices  221 us (37%)
  blocking collectives  121 us (20%)
  local copies, waits for them, and re-layouts  96 us (16%)
  starting transfers between devices  55.3 us (9%)
  other arithmetic  46.1 us (8%)
  matrix products  39 us (6%)
  between operations  15.2 us (3%)
    all_gather x5, waiting for transfers between devices, by_axis(): x = jnp.sum(lax.all_gather(x, axis), axis=0)  142 us
    all_gather x10, blocking collectives, by_axis(): x = jnp.sum(lax.all_gather(x, axis), axis=0)  121 us
    mul x3, local copies, waits for them, and re-layouts, apply_local(): widened = jnp.kron(unitary, jnp.eye(4, dtype=unitary.dtype))  57.7 us
    all_to_all x1, waiting for transfers between devices, side_by_side(): lax.all_to_all(both, axis, split_axis=split_dim, concat_axis=concat_dim,...  51.8 us
    all_to_all x1, starting transfers between devices, on_device(): lax.all_to_all(current, AMP, split_axis=1, concat_axis=0, tiled=True)  31 us
    all_to_all x1, waiting for transfers between devices, on_device(): lax.all_to_all(current, AMP, split_axis=1, concat_axis=0, tiled=True)  26.4 us
    mul x1, other arithmetic, apply_local(): widened = jnp.kron(unitary, jnp.eye(4, dtype=unitary.dtype))  22.1 us
    ppermute x5, starting transfers between devices, swapped(): lax.ppermute(x, axis, [(i, i ^ 1 << bit) for i in range(lax.axis_size(axi...  14.6 us
  transfers between devices with their start and end apart: 12, of which 6 were waited for; matrix products, arithmetic and copies ran while one was open for 15% of the time, Pallas kernels for 0%

profile of v1, /device:TPU:33, one launch (start us, length us, event | category | flops | bytes accessed | tf_op | source)
XLA Modules:
  0.0 593.0 jit_solution(8881587329077863694)
XLA Ops:
  9.1 5.6 select_add_fusion
  14.6 3.1 fusion.1
  17.8 1.5 fusion.4
  20.6 22.1 %broadcast_multiply_fusion.1 = (f32[128,4,128,4]{3,2,1,0:T(8,128)}, f32[128,4,128,4]{3,2,1,0:T(8,128)}) fusion(f32[4,4]{1,0:T(4,128)S(1)} %fusion.178, f32[128,128]{1,0:T(8,128)S(1)} %get-tuple-element.4, f32[128,128]{1,0:T(8,128)S(1)} %copy.171), kind=kLoop, calls=%fused_computation.1 | loop fusion | flops 524288 | bytes 2228288 | tf_op jit(solution)/shard_map/jit(kron)/mul | solution.py:82
  42.7 29.0 %reshape.506 = f32[4,128,512,1]{2,1,0,3:T(8,128)S(1)} reshape(f32[128,4,128,4]{3,2,1,0:T(8,128)} %get-tuple-element.15) | data formatting | bytes 2097152 | tf_op jit(solution)/shard_map/jit(kron)/mul | solution.py:82
  72.5 1.1 fusion.22
  74.2 1.1 copy.143
  75.3 31.0 %all-to-all-start = ((f32[1,1024,128]{2,0,1:T(1,128)}), f32[1,1024,128]{2,0,1:T(1,128)S(1)}, u32[]{:S(2)}, u32[]{:S(2)}) async-start(f32[1,1024,128]{2,0,1:T(1,128)} %bitcast.16), calls=%async_computation | async-start | bytes 1048576 | tf_op jit(solution)/shard_map/all_to_all | solution.py:197
  110.7 26.4 %all-to-all-done = f32[1,1024,128]{2,0,1:T(1,128)S(1)} async-done(((f32[1,1024,128]{2,0,1:T(1,128)}), f32[1,1024,128]{2,0,1:T(1,128)S(1)}, u32[]{:S(2)}, u32[]{:S(2)}) %all-to-all-start) | async-done | bytes 524320 | tf_op jit(solution)/shard_map/all_to_all | solution.py:197
  137.7 1.0 fusion.31
  138.9 1.1 reshape_reshape_reshape.16
  140.0 1.1 reshape_reshape_reshape.17
  141.2 1.1 reshape_reshape_reshape.18
  142.6 3.3 fusion.29
  146.8 5.1 convolution_bitcast_fusion.3
  153.2 1.3 constant_dynamic-slice_fusion.2
  155.4 1.3 constant_dynamic-slice_fusion.1
  157.6 1.9 collective-permute-start.2
  160.6 2.9 collective-permute-start.3
  164.5 9.1 %collective-permute-start.4 = (f32[1,65536]{1,0:T(1,128)}, f32[1,65536]{1,0:T(1,128)S(1)}, u32[]{:S(2)}, u32[]{:S(2)}) collective-permute-start(f32[1,65536]{1,0:T(1,128)} %dynamic-slice_bitcast_fusion), channel_id=1, source_target_pairs={{0,8},{1,9},{2,10},{3,11},{4,12},{5,13},{6,14},{7,15},{8,0},{9,1},... | collective-permute-start | bytes 786440 | tf_op jit(solution)/shard_map/ppermute | solution.py:16
  173.6 5.7 fusion.39
  182.6 1.6 broadcast_multiply_fusion.4
  184.6 2.8 dynamic_update_slice.21
  188.0 1.6 broadcast_multiply_fusion.3
  190.0 3.3 dynamic_update_slice.22
  194.0 1.7 broadcast_multiply_fusion.2
  196.0 3.3 dynamic_update_slice.23
  200.9 3.3 dynamic_update_slice.24
  206.2 1.1 pad_maximum_fusion
  207.3 9.2 %all-to-all-start.1 = ((f32[128,8,256]{2,1,0:T(8,128)}), f32[128,8,256]{2,1,0:T(8,128)}, u32[]{:S(2)}, u32[]{:S(2)}) async-start(f32[128,8,256]{2,1,0:T(8,128)} %pad_maximum_fusion), calls=%async_computation.1 | async-start | bytes 2097152 | tf_op jit(solution)/shard_map/all_to_all | solution.py:22
  216.6 1.2 convolution_bitcast_fusion.6
  217.9 1.2 convolution_bitcast_fusion.7
  219.3 51.8 %all-to-all-done.1 = f32[128,8,256]{2,1,0:T(8,128)} async-done(((f32[128,8,256]{2,1,0:T(8,128)}), f32[128,8,256]{2,1,0:T(8,128)}, u32[]{:S(2)}, u32[]{:S(2)}) %all-to-all-start.1) | async-done | bytes 1048608 | tf_op jit(solution)/shard_map/all_to_all | solution.py:22
  271.1 1.3 fusion.206
  272.4 1.0 fusion.27
  273.4 1.3 convolution_bitcast_fusion.8
  274.8 28.7 %mul.219 = f32[512,512]{1,0:T(8,128)S(1)} reshape(f32[128,4,128,4]{3,2,1,0:T(8,128)} %get-tuple-element.16) | data formatting | bytes 2097152 | tf_op jit(solution)/shard_map/jit(kron)/mul | solution.py:82
  303.8 1.1 fusion.10
  305.2 1.0 convolution_bitcast_fusion.1
  306.2 1.2 copy.174
  307.4 1.6 reshape.486
  309.0 1.3 convolution_bitcast_fusion.9
  310.9 1.1 fusion.13
  312.6 1.6 fusion.211
  314.3 1.3 reduce_sum.147
  315.6 14.0 %all-gather.13 = f32[512,128]{1,0:T(8,128)S(1)} all-gather(f32[128,128]{1,0:T(8,128)S(1)} %reduce_sum.147), channel_id=15, replica_groups=mesh['runs'=2,'amp_0'=16,'amp_1'=4,'amp_2'=2] {'amp_1'}, dimensions={0}, use_global_device_ids=true | all-gather | bytes 327680 | tf_op jit(solution)/shard_map/all_gather | solution.py:28
  329.6 4.1 all-gather.14
  333.7 20.6 %all-gather.27.cloned.1.call-done = f32[2048,128]{1,0:T(8,128)} async-done(((f32[128,128]{1,0:T(8,128)}), f32[2048,128]{1,0:T(8,128)}) %all-gather.27.cloned.1.call-update) | async-done | bytes 1048592 | tf_op jit(solution)/shard_map/all_gather | solution.py:28
  354.3 1.3 reduce_sum.144
  355.6 10.2 %all-gather.10 = f32[512,128]{1,0:T(8,128)S(1)} all-gather(f32[128,128]{1,0:T(8,128)S(1)} %reduce_sum.144), channel_id=12, replica_groups=mesh['runs'=2,'amp_0'=16,'amp_1'=4,'amp_2'=2] {'amp_1'}, dimensions={0}, use_global_device_ids=true | all-gather | bytes 327680 | tf_op jit(solution)/shard_map/all_gather | solution.py:28
  365.9 15.1 %all-gather.11 = f32[256,128]{1,0:T(8,128)S(1)} all-gather(f32[128,128]{1,0:T(8,128)S(1)} %reduce_sum.145), channel_id=13, replica_groups=mesh['runs'=2,'amp_0'=16,'amp_1'=4,'amp_2'=2] {'amp_2'}, dimensions={0}, use_global_device_ids=true | all-gather | bytes 196608 | tf_op jit(solution)/shard_map/all_gather | solution.py:28
  380.9 1.4 convolution_bitcast_fusion
  382.3 39.8 %all-gather.25.cloned.1.call-done = f32[2048,128]{1,0:T(8,128)} async-done(((f32[128,128]{1,0:T(8,128)}), f32[2048,128]{1,0:T(8,128)}) %all-gather.25.cloned.1.call-update) | async-done | bytes 1048592 | tf_op jit(solution)/shard_map/all_gather | solution.py:28
  422.0 1.3 reduce_sum.141
  423.3 10.5 %all-gather.7 = f32[512,128]{1,0:T(8,128)S(1)} all-gather(f32[128,128]{1,0:T(8,128)S(1)} %reduce_sum.141), channel_id=9, replica_groups=mesh['runs'=2,'amp_0'=16,'amp_1'=4,'amp_2'=2] {'amp_1'}, dimensions={0}, use_global_device_ids=true | all-gather | bytes 327680 | tf_op jit(solution)/shard_map/all_gather | solution.py:28
  433.9 15.3 %all-gather.8 = f32[256,128]{1,0:T(8,128)S(1)} all-gather(f32[128,128]{1,0:T(8,128)S(1)} %reduce_sum.142), channel_id=10, replica_groups=mesh['runs'=2,'amp_0'=16,'amp_1'=4,'amp_2'=2] {'amp_2'}, dimensions={0}, use_global_device_ids=true | all-gather | bytes 196608 | tf_op jit(solution)/shard_map/all_gather | solution.py:28
  449.2 40.7 %all-gather.23.cloned.1.call-done = f32[2048,128]{1,0:T(8,128)} async-done(((f32[128,128]{1,0:T(8,128)}), f32[2048,128]{1,0:T(8,128)}) %all-gather.23.cloned.1.call-update) | async-done | bytes 1048592 | tf_op jit(solution)/shard_map/all_gather | solution.py:28
  489.8 1.3 reduce_sum.138
  491.1 10.5 %all-gather.4 = f32[512,128]{1,0:T(8,128)S(1)} all-gather(f32[128,128]{1,0:T(8,128)S(1)} %reduce_sum.138), channel_id=6, replica_groups=mesh['runs'=2,'amp_0'=16,'amp_1'=4,'amp_2'=2] {'amp_1'}, dimensions={0}, use_global_device_ids=true | all-gather | bytes 327680 | tf_op jit(solution)/shard_map/all_gather | solution.py:28
  501.7 15.2 %all-gather.5 = f32[256,128]{1,0:T(8,128)S(1)} all-gather(f32[128,128]{1,0:T(8,128)S(1)} %reduce_sum.139), channel_id=7, replica_groups=mesh['runs'=2,'amp_0'=16,'amp_1'=4,'amp_2'=2] {'amp_2'}, dimensions={0}, use_global_device_ids=true | all-gather | bytes 196608 | tf_op jit(solution)/shard_map/all_gather | solution.py:28
  516.9 41.4 %all-gather.21.cloned.1.call-done = f32[2048,128]{1,0:T(8,128)} async-done(((f32[128,128]{1,0:T(8,128)}), f32[2048,128]{1,0:T(8,128)}) %all-gather.21.cloned.1.call-update) | async-done | bytes 1048592 | tf_op jit(solution)/shard_map/all_gather | solution.py:28
  558.2 1.3 reduce_sum.135
  559.5 10.5 %all-gather.1 = f32[512,128]{1,0:T(8,128)S(1)} all-gather(f32[128,128]{1,0:T(8,128)S(1)} %reduce_sum.135), channel_id=3, replica_groups=mesh['runs'=2,'amp_0'=16,'amp_1'=4,'amp_2'=2] {'amp_1'}, dimensions={0}, use_global_device_ids=true | all-gather | bytes 327680 | tf_op jit(solution)/shard_map/all_gather | solution.py:28
  570.0 15.2 %all-gather.2 = f32[256,128]{1,0:T(8,128)S(1)} all-gather(f32[128,128]{1,0:T(8,128)S(1)} %reduce_sum.136), channel_id=4, replica_groups=mesh['runs'=2,'amp_0'=16,'amp_1'=4,'amp_2'=2] {'amp_2'}, dimensions={0}, use_global_device_ids=true | all-gather | bytes 196608 | tf_op jit(solution)/shard_map/all_gather | solution.py:28
  (140 shorter events, 28.2 us)
Async XLA Ops:
  7.2 64.5 %copy-start = (f32[1,1024,128]{2,1,0:T(8,128)S(1)}, f32[1,1024,128]{2,1,0:T(8,128)}, u32[]{:S(2)}) copy-start(f32[1,1024,128]{2,1,0:T(8,128)} %param.5) | copy-start | bytes 1572868
  72.5 36.8 %copy-start.4 = (f32[23]{0:T(128)S(1)}, f32[23]{0:T(128)}, u32[]{:S(2)}) copy-start(f32[23]{0:T(128)} %param.8) | copy-start | bytes 280
  72.5 36.8 %copy-start.5 = (s32[23]{0:T(128)S(1)}, s32[23]{0:T(128)}, u32[]{:S(2)}) copy-start(s32[23]{0:T(128)} %param.9) | copy-start | bytes 280
  75.3 61.7 %all-to-all-start = ((f32[1,1024,128]{2,0,1:T(1,128)}), f32[1,1024,128]{2,0,1:T(1,128)S(1)}, u32[]{:S(2)}, u32[]{:S(2)}) async-start(f32[1,1024,128]{2,0,1:T(1,128)} %bitcast.16), calls=%async_computation | async-start | bytes 1048576 | tf_op jit(solution)/shard_map/all_to_all | solution.py:197
  152.2 7.2 %copy-start.2 = (f32[2,2,32768]{2,1,0:T(2,128)S(1)}, f32[2,2,32768]{2,1,0:T(2,128)}, u32[]{:S(2)}) copy-start(f32[2,2,32768]{2,1,0:T(2,128)} %reshape_reshape_reshape.18) | copy-start | bytes 1572868
  152.2 21.4 %copy-start.6 = (s32[256]{0:T(256)S(1)}, s32[256]{0:T(256)}, u32[]{:S(2)}) copy-start(s32[256]{0:T(256)} %iota_xor_fusion.7) | copy-start | bytes 3076
  152.2 21.4 %copy-start.7 = (pred[256]{0:T(512)(128)(4,1)S(1)}, pred[256]{0:T(512)(128)(4,1)}, u32[]{:S(2)}) copy-start(pred[256]{0:T(512)(128)(4,1)} %get-tuple-element.60) | copy-start | bytes 772
  152.2 21.3 %copy-start.8 = (pred[256]{0:T(512)(128)(4,1)S(1)}, pred[256]{0:T(512)(128)(4,1)}, u32[]{:S(2)}) copy-start(pred[256]{0:T(512)(128)(4,1)} %get-tuple-element.61) | copy-start | bytes 772
  152.3 21.3 %copy-start.9 = (pred[256]{0:T(512)(128)(4,1)S(1)}, pred[256]{0:T(512)(128)(4,1)}, u32[]{:S(2)}) copy-start(pred[256]{0:T(512)(128)(4,1)} %get-tuple-element.64) | copy-start | bytes 772
  152.3 21.3 %copy-start.10 = (pred[256]{0:T(512)(128)(4,1)S(1)}, pred[256]{0:T(512)(128)(4,1)}, u32[]{:S(2)}) copy-start(pred[256]{0:T(512)(128)(4,1)} %get-tuple-element.65) | copy-start | bytes 772
  152.3 21.3 %copy-start.11 = (pred[256]{0:T(512)(128)(4,1)S(1)}, pred[256]{0:T(512)(128)(4,1)}, u32[]{:S(2)}) copy-start(pred[256]{0:T(512)(128)(4,1)} %get-tuple-element.68) | copy-start | bytes 772
  152.3 21.3 %copy-start.12 = (pred[256]{0:T(512)(128)(4,1)S(1)}, pred[256]{0:T(512)(128)(4,1)}, u32[]{:S(2)}) copy-start(pred[256]{0:T(512)(128)(4,1)} %get-tuple-element.69) | copy-start | bytes 772
  152.3 21.3 %copy-start.13 = (pred[256]{0:T(512)(128)(4,1)S(1)}, pred[256]{0:T(512)(128)(4,1)}, u32[]{:S(2)}) copy-start(pred[256]{0:T(512)(128)(4,1)} %fusion.186) | copy-start | bytes 772
  152.6 28.4 %collective-permute-start = (f32[128,512]{0,1:T(8,128)S(1)}, f32[128,512]{0,1:T(8,128)S(1)}, u32[]{:S(2)}, u32[]{:S(2)}) collective-permute-start(f32[128,512]{0,1:T(8,128)S(1)} %dynamic-slice_bitcast_fusion.1), channel_id=1, source_target_pairs={{0,1},{1,0},{2,3},{3,2},{4,5},{5,4},{6,7},{7,6},{8,9},{9,8},{10,11... | collective-permute-start | bytes 786440 | tf_op jit(solution)/shard_map/ppermute | solution.py:16
  155.4 27.3 %collective-permute-start.1 = (f32[8,8192]{1,0:T(8,128)}, f32[8,8192]{1,0:T(8,128)}, u32[]{:S(2)}, u32[]{:S(2)}) collective-permute-start(f32[8,8192]{1,0:T(8,128)} %bitcast.250), channel_id=1, source_target_pairs={{0,1},{1,0},{2,3},{3,2},{4,5},{5,4},{6,7},{7,6},{8,9},{9,8},{10,11... | collective-permute-start | bytes 786440 | tf_op jit(solution)/shard_map/ppermute | solution.py:16
  157.6 30.4 %collective-permute-start.2 = (f32[4,16384]{1,0:T(4,128)}, f32[4,16384]{1,0:T(4,128)}, u32[]{:S(2)}, u32[]{:S(2)}) collective-permute-start(f32[4,16384]{1,0:T(4,128)} %bitcast.249), channel_id=1, source_target_pairs={{0,2},{1,3},{2,0},{3,1},{4,6},{5,7},{6,4},{7,5},{8,10},{9,11},{10,... | collective-permute-start | bytes 786440 | tf_op jit(solution)/shard_map/ppermute | solution.py:16
  160.6 33.3 %collective-permute-start.3 = (f32[2,32768]{1,0:T(2,128)}, f32[2,32768]{1,0:T(2,128)}, u32[]{:S(2)}, u32[]{:S(2)}) collective-permute-start(f32[2,32768]{1,0:T(2,128)} %bitcast.248), channel_id=1, source_target_pairs={{0,4},{1,5},{2,6},{3,7},{4,0},{5,1},{6,2},{7,3},{8,12},{9,13},{10,... | collective-permute-start | bytes 786440 | tf_op jit(solution)/shard_map/ppermute | solution.py:16
  164.5 35.5 %collective-permute-start.4 = (f32[1,65536]{1,0:T(1,128)}, f32[1,65536]{1,0:T(1,128)S(1)}, u32[]{:S(2)}, u32[]{:S(2)}) collective-permute-start(f32[1,65536]{1,0:T(1,128)} %dynamic-slice_bitcast_fusion), channel_id=1, source_target_pairs={{0,8},{1,9},{2,10},{3,11},{4,12},{5,13},{6,14},{7,15},{8,0},{9,1},... | collective-permute-start | bytes 786440 | tf_op jit(solution)/shard_map/ppermute | solution.py:16
  207.3 63.8 %all-to-all-start.1 = ((f32[128,8,256]{2,1,0:T(8,128)}), f32[128,8,256]{2,1,0:T(8,128)}, u32[]{:S(2)}, u32[]{:S(2)}) async-start(f32[128,8,256]{2,1,0:T(8,128)} %pad_maximum_fusion), calls=%async_computation.1 | async-start | bytes 2097152 | tf_op jit(solution)/shard_map/all_to_all | solution.py:22
  216.5 97.8 %all-gather.29.cloned.1.call-start = ((), (), s32[]{:S(2)}) async-start(), calls=%async_computation.6 | async-start | bytes 1114112 | tf_op jit(solution)/shard_map/all_gather | solution.py:28
  217.9 136.4 %all-gather.27.cloned.1.call-start = ((), (), s32[]{:S(2)}) async-start(), calls=%async_computation.5 | async-start | bytes 1114112 | tf_op jit(solution)/shard_map/all_gather | solution.py:28
  219.2 202.8 %all-gather.25.cloned.1.call-start = ((), (), s32[]{:S(2)}) async-start(), calls=%async_computation.4 | async-start | bytes 1114112 | tf_op jit(solution)/shard_map/all_gather | solution.py:28
  274.8 215.1 %all-gather.23.cloned.1.call-start = ((), (), s32[]{:S(2)}) async-start(), calls=%async_computation.3 | async-start | bytes 1114112 | tf_op jit(solution)/shard_map/all_gather | solution.py:28
  310.3 247.9 %all-gather.21.cloned.1.call-start = ((), (), s32[]{:S(2)}) async-start(), calls=%async_computation.2 | async-start | bytes 1114112 | tf_op jit(solution)/shard_map/all_gather | solution.py:28
  433.9 152.2 %copy-start.1 = (f32[1,1024,128]{2,1,0:T(8,128)S(1)}, f32[1,1024,128]{2,1,0:T(8,128)}, u32[]{:S(2)}) copy-start(f32[1,1024,128]{2,1,0:T(8,128)} %param.5) | copy-start | bytes 1572868
  585.3 0.7 copy-start.3
Sparse Core Ops, SparseCore 0:
  219.1 72.1 all-gather.28
  293.2 61.1 all-gather.26
  356.1 65.8 all-gather.24
  423.7 66.1 all-gather.22
  492.1 66.1 all-gather.20
